TPU v7x, 32 devices: a whole 2x2x4 slice. The times are simulated.
32 devices in a mesh: groups: 2 (over y), rows: 4 (over z), cols: 2 (over x), sub: 2 (over core).
Axes of the slice: x: 2, y: 2, z: 4, core: 2. Of those that a mesh axis runs over, the one named last changes fastest.
Arguments:
- stored_vectors: bfloat16 [3072, 8192], P(('cols', 'sub'), ('groups', 'rows')), parts along dimension 1, may hold values from -0.59765625 to 0.59765625
- previous_columns: bfloat16 [8192, 256], P(('groups', 'rows', 'cols', 'sub')), parts along dimension 0, may hold values from -3 to 3
- pivots: int32 [512], P('groups'), parts along dimension 0, may hold values from 0 to 4095, as said below
- diagonal: float32 [8192], P(('groups', 'rows', 'cols', 'sub')), parts along dimension 0, may hold values from 2 to 32
- ket_blocks: bfloat16 [128, 128, 256], P(('groups', 'rows', 'cols', 'sub')), parts along dimension 0, may hold values from -6 to 6
- shell_tags: int32 [128, 128], P(('groups', 'rows', 'cols', 'sub')), parts along dimension 0, may hold values from 0 to 3
- target_blocks: int32 [32, 4], P('groups'), parts along dimension 0, may hold values from 0 to 31, as said below
- block_counts: int32 [32], P('groups'), parts along dimension 0, may hold values from 0 to 4, as said below
- shell_norms: float32 [4], replicated, may hold values from 0.5 to 2
Outputs:
- new_vectors: bfloat16 [8192, 256], P(('groups', 'rows', 'cols', 'sub')), parts along dimension 0
- diag_out: float32 [8192], P(('groups', 'rows', 'cols', 'sub')), parts along dimension 0
- next_columns: bfloat16 [8192, 256], P(('groups', 'rows', 'cols', 'sub')), parts along dimension 0
There are 2 independent parts, one for each index of `groups`. A program takes and returns all parts, laid end to end along the dimension named above; an argument that names none is the same for every part. Nothing has to cross between parts.
Inputs may be any that keep to these rules, and one draw needn't show every extreme that they name: `pivots`: 256 distinct AO pairs. `target_blocks`: the used slots of all owners name every block of the 32 blocks exactly once; a used slot's block lies on a device with the owner's cols and sub indices (blocks g * 2 to g * 2 + 1 lie on the device of linear index g, rows slowest; owner o is the device of linear index o). At most 1 of one owner's used slots go to one device, and some owner reaches that in every draw. Entries of unused slots are arbitrary blocks. `block_counts`: some owner uses all 4 slots in every draw.
All inputs are finite; a program needn't handle non-finite values.
Results may differ from a plain program's by a relative error of at most 0.0004.
Values may be sent and summed in bfloat16 or wider, within the bound.
A program may use at most 64 MiB of HBM per device.

v0:
```python
import jax
import jax.numpy as jnp
from jax import lax
from jax.sharding import PartitionSpec as P


def slot_plan(row_targets, count, column_size, per_device):
    slot_count = row_targets.shape[0]
    slots = jnp.arange(slot_count, dtype=jnp.int32)
    valid = slots < count
    receiver = row_targets // (column_size * per_device)
    within = row_targets % per_device
    earlier = (
        (receiver[:, None] == receiver[None, :])
        & valid[:, None]
        & valid[None, :]
        & (slots[None, :] < slots[:, None])
    )
    ranking = jnp.sum(earlier.astype(jnp.int32), axis=1)
    return (valid, receiver, ranking, within)


def body(
    stored_vectors,
    previous_columns,
    pivots,
    diagonal,
    ket_blocks,
    shell_tags,
    target_blocks,
    block_counts,
    shell_norms,
):
    rows_here = previous_columns.shape[0]
    batch = previous_columns.shape[1]
    block_rows = ket_blocks.shape[1]
    slot_count = ket_blocks.shape[0]
    per_device = rows_here // block_rows
    band_rows = stored_vectors.shape[1]
    band_index = lax.axis_index("rows")
    device_index = lax.axis_index(("rows", "cols", "sub"))
    column_index = lax.axis_index(("cols", "sub"))
    column_size = lax.axis_size(("cols", "sub"))
    band_size = lax.axis_size("rows")
    peer_slots = (slot_count + band_size - 1) // band_size
    local_pivots = pivots - device_index * rows_here
    matches = jnp.arange(rows_here, dtype=jnp.int32)[:, None] == local_pivots[None, :]
    diag_terms = jnp.sum(jnp.where(matches, diagonal[:, None], jnp.float32(0.0)), axis=0)
    pivot_diag = lax.psum(diag_terms, ("rows", "cols", "sub"))
    band_pivots = pivots - band_index * band_rows
    inside = (band_pivots >= 0) & (band_pivots < band_rows)
    clamped = jnp.clip(band_pivots, 0, band_rows - 1)
    taken = jnp.take(stored_vectors, clamped, axis=1).astype(jnp.float32)
    picked = jnp.where(inside[None, :], taken, jnp.float32(0.0))
    pivot_rows = lax.psum(picked, "rows").astype(jnp.bfloat16)
    kinds = jnp.arange(shell_norms.shape[0], dtype=jnp.int32)
    factor = jnp.sum(
        jnp.where(shell_tags[..., None] == kinds, shell_norms, jnp.float32(0.0)), axis=-1
    )
    fresh = (ket_blocks.astype(jnp.float32) * factor[..., None]).astype(jnp.bfloat16)
    own_targets = lax.dynamic_index_in_dim(target_blocks, device_index, 0, keepdims=False)
    own_count = lax.dynamic_index_in_dim(block_counts, device_index, 0, keepdims=False)
    valid, receiver, ranking, within = slot_plan(own_targets, own_count, column_size, per_device)
    lines = jnp.arange(band_size * peer_slots, dtype=jnp.int32)[:, None]
    routing = (
        (lines // peer_slots == receiver[None, :])
        & (lines % peer_slots == ranking[None, :])
        & valid[None, :]
    ).astype(jnp.bfloat16)
    outgoing = jnp.dot(
        routing, fresh.reshape(slot_count, block_rows * batch), preferred_element_type=jnp.float32
    )
    outgoing = outgoing.astype(jnp.bfloat16).reshape(band_size, peer_slots, block_rows, batch)
    incoming = lax.all_to_all(outgoing, "rows", split_axis=0, concat_axis=0, tiled=True)
    sources = jnp.arange(band_size, dtype=jnp.int32) * column_size + column_index
    source_targets = jnp.take(target_blocks, sources, axis=0)
    source_counts = jnp.take(block_counts, sources, axis=0)
    plan_each = jax.vmap(
        lambda row_targets, count: slot_plan(row_targets, count, column_size, per_device)
    )
    source_valid, source_receiver, source_rank, source_within = plan_each(
        source_targets, source_counts
    )
    arriving = source_valid & (source_receiver == band_index)
    places = jnp.arange(per_device, dtype=jnp.int32)[:, None, None, None]
    peer_lines = jnp.arange(peer_slots, dtype=jnp.int32)[None, None, :, None]
    hits = (
        (source_within[None, :, None, :] == places)
        & (source_rank[None, :, None, :] == peer_lines)
        & arriving[None, :, None, :]
    )
    placement = (
        jnp.any(hits, axis=3).astype(jnp.bfloat16).reshape(per_device, band_size * peer_slots)
    )
    arranged = jnp.dot(
        placement,
        incoming.reshape(band_size * peer_slots, block_rows * batch),
        preferred_element_type=jnp.float32,
    )
    next_columns = arranged.astype(jnp.bfloat16).reshape(rows_here, batch)
    product = lax.psum_scatter(
        lax.dot_general(
            stored_vectors, pivot_rows, (((0,), (0,)), ((), ())), preferred_element_type=jnp.float32
        ),
        ("cols", "sub"),
        scatter_dimension=0,
        tiled=True,
    )
    residual_cols = previous_columns.astype(jnp.float32) - product
    scaled = residual_cols / jnp.sqrt(pivot_diag)[None, :]
    new_vectors = scaled.astype(jnp.bfloat16)
    diag_out = diagonal - jnp.sum(scaled * scaled, axis=1)
    return (new_vectors, diag_out, next_columns)


def solution(mesh):
    return jax.shard_map(
        body,
        mesh=mesh,
        in_specs=(
            P(("cols", "sub"), ("groups", "rows")),
            P(("groups", "rows", "cols", "sub"), None),
            P("groups"),
            P(("groups", "rows", "cols", "sub")),
            P(("groups", "rows", "cols", "sub"), None, None),
            P(("groups", "rows", "cols", "sub"), None),
            P("groups", None),
            P("groups"),
            P(),
        ),
        out_specs=(
            P(("groups", "rows", "cols", "sub"), None),
            P(("groups", "rows", "cols", "sub")),
            P(("groups", "rows", "cols", "sub"), None),
        ),
        check_vma=False,
    )
```

profile of v0, /device:TPU:0, one launch (start us, length us, event | category | flops | bytes accessed | tf_op | source)
XLA Modules:
  0.0 100.1 jit_solution(16816415105481037228)
XLA Ops:
  7.2 0.0 reduce-scatter.2.cloned.1.call-start
  7.2 0.0 copy-start.6
  7.2 1.7 %copy.26 = bf16[768,1024]{0,1:T(8,128)(2,1)S(1)} copy(bf16[768,1024]{1,0:T(8,128)(2,1)} %param.9) | data formatting | bytes 3145728 | tf_op args[0]
  9.0 0.0 copy-done.6
  9.0 1.2 %gather_fusion = bf16[256,768]{1,0:T(8,128)(2,1)S(1)} fusion(bf16[768,1024]{0,1:T(8,128)(2,1)S(1)} %copy.26, s32[1024]{0:T(1024)S(1)} %pad_clamp_fusion.1), kind=kCustom, calls=%fused_computation | custom fusion | bytes 787456 | tf_op jit(solution)/shard_map/jit(_take)/gather | solution.py:53
  10.2 0.0 copy-start.1
  10.2 0.2 select_bitcast_fusion
  10.4 37.4 %all-reduce.1 = bf16[768,256]{0,1:T(8,128)(2,1)S(1)} all-reduce(f32[768,256]{0,1:T(8,128)S(1)} %select_bitcast_fusion), channel_id=1, replica_groups=mesh['groups'=2,'rows'=4,'cols'=2,'sub'=2] {'rows'}, use_global_device_ids=true, to_apply=%region_0.1 | all-reduce | flops 196608 | bytes 1179648 | tf_op jit(solution)/shard_map/psum | solution.py:55
  47.8 0.0 copy-done.1
  47.8 0.0 copy-start.7
  47.8 0.0 copy-start.8
  47.9 0.0 copy-start.2
  47.9 1.6 %convolution_bitcast_fusion = f32[1024,256]{0,1:T(8,128)} fusion(bf16[768,1024]{1,0:T(8,128)(2,1)S(1)} %copy-done.1, bf16[768,256]{0,1:T(8,128)(2,1)S(1)} %all-reduce.1), kind=kOutput, calls=%fused_computation.5 | convolution fusion | flops 402653184 | bytes 3014656 | tf_op jit(solution)/shard_map/dot_general | solution.py:102
  49.4 0.0 copy-start.4
  49.4 0.0 copy-start
  49.4 0.0 reduce-scatter.2.cloned.1.call-update
  49.5 0.0 copy-done.7
  49.5 0.0 copy-done.8
  49.5 0.1 select_reduce_fusion.1
  49.6 0.0 copy-done.2
  49.6 0.0 copy-start.5
  49.6 0.0 copy-start.3
  49.6 0.1 fusion.1
  49.7 0.2 copy.30
  50.0 0.2 copy-done.4
  50.1 0.2 dynamic-slice_reduce_fusion
  50.3 0.0 copy-done
  50.3 0.6 dynamic_slice.9
  50.9 0.6 iota_compare_fusion.6
  51.6 0.2 convert_reduce_fusion.1
  51.8 0.3 convolution_convert_fusion
  52.1 0.7 copy.34
  52.8 3.4 %all-to-all-start = ((bf16[4,1,128,256]{3,2,1,0:T(8,128)(2,1)}), bf16[4,1,128,256]{3,2,1,0:T(8,128)(2,1)S(1)}, u32[]{:S(2)}, u32[]{:S(2)}) async-start(bf16[4,1,128,256]{3,2,1,0:T(8,128)(2,1)} %bitcast.26), calls=%async_computation.1 | async-start | bytes 524288 | tf_op jit(solution)/shard_map/all_to_all | solution.py:74
  56.2 0.1 copy.27
  56.3 0.6 gather_fusion.2
  57.0 0.6 gather_fusion.1
  57.6 0.1 compare_and_fusion
  57.6 0.2 convert_reduce_fusion
  57.9 0.0 copy-done.5
  57.9 0.1 select_reduce_fusion
  58.0 31.2 %psum.15 = f32[256]{0:T(256)S(1)} all-reduce(f32[256]{0:T(256)S(1)} %select_reduce_fusion), channel_id=1, replica_groups=mesh['groups'=2,'rows'=4,'cols'=2,'sub'=2] {'rows','cols','sub'}, use_global_device_ids=true, to_apply=%region_3.4 | all-reduce | flops 256 | bytes 2048 | tf_op jit(solution)/shard_map/psum | solution.py:49
  89.2 0.0 copy-done.3
  89.2 0.1 copy.25
  89.3 0.1 add_select_fusion.2
  89.4 0.2 fusion.4
  89.5 0.0 all-to-all-done
  89.6 0.2 copy.32
  89.8 0.3 convolution_convert_fusion.1
  90.1 0.7 reshape.328
  90.8 0.0 reduce-scatter.2.cloned.1.call-done
  90.8 1.1 %multiply_reduce_fusion = (f32[256]{0:T(256)S(1)}, bf16[256,256]{0,1:T(8,128)(2,1)S(1)}) fusion(f32[256]{0:T(256)S(1)} %sqrt.3, f32[256,256]{0,1:T(8,128)} %reduce-scatter.2.cloned.1.call-done, bf16[256,256]{0,1:T(8,128)(2,1)S(1)} %copy.25), kind=kLoop, calls=%fused_computation.11 | loop fusion | flops 392960 | bytes 526336 | tf_op jit(solution)/shard_map/reduce_sum | solution.py:112
  91.9 0.8 copy.29
  92.6 0.6 sub.35
  (11 shorter events, 0.1 us)
Async XLA Ops:
  7.2 83.6 %reduce-scatter.2.cloned.1.call-start = ((), (), s32[]{:S(2)}) async-start(), calls=%async_computation.2 | async-start | bytes 1310720 | tf_op jit(solution)/shard_map/reduce_scatter | solution.py:101
  7.2 1.7 %copy-start.6 = (s32[256]{0:T(256)S(1)}, s32[256]{0:T(256)}, u32[]{:S(2)}) copy-start(s32[256]{0:T(256)} %param.11) | copy-start | bytes 3076
  10.2 37.6 %copy-start.1 = (bf16[768,1024]{1,0:T(8,128)(2,1)S(1)}, bf16[768,1024]{1,0:T(8,128)(2,1)}, u32[]{:S(2)}) copy-start(bf16[768,1024]{1,0:T(8,128)(2,1)} %param.9) | copy-start | bytes 4718596
  47.8 1.6 %copy-start.7 = (s32[4,128]{1,0:T(4,128)S(1)}, s32[4,128]{1,0:T(4,128)}, u32[]{:S(2)}) copy-start(s32[4,128]{1,0:T(4,128)} %param.14) | copy-start | bytes 6148
  47.8 1.6 %copy-start.8 = (f32[4]{0:T(128)S(1)}, f32[4]{0:T(128)}, u32[]{:S(2)}) copy-start(f32[4]{0:T(128)} %param.17) | copy-start | bytes 52
  47.9 1.7 %copy-start.2 = (bf16[4,128,256]{2,1,0:T(8,128)(2,1)S(1)}, bf16[4,128,256]{2,1,0:T(8,128)(2,1)}, u32[]{:S(2)}) copy-start(bf16[4,128,256]{2,1,0:T(8,128)(2,1)} %param.13) | copy-start | bytes 786436
  49.4 0.7 copy-start.4
  49.4 0.9 copy-start
  49.6 8.3 %copy-start.5 = (f32[256]{0:T(256)S(1)}, f32[256]{0:T(256)}, u32[]{:S(2)}) copy-start(f32[256]{0:T(256)} %param.12) | copy-start | bytes 3076
  49.6 39.6 %copy-start.3 = (bf16[256,256]{1,0:T(8,128)(2,1)S(1)}, bf16[256,256]{1,0:T(8,128)(2,1)}, u32[]{:S(2)}) copy-start(bf16[256,256]{1,0:T(8,128)(2,1)} %param.10) | copy-start | bytes 393220
  52.8 36.7 %all-to-all-start = ((bf16[4,1,128,256]{3,2,1,0:T(8,128)(2,1)}), bf16[4,1,128,256]{3,2,1,0:T(8,128)(2,1)S(1)}, u32[]{:S(2)}, u32[]{:S(2)}) async-start(bf16[4,1,128,256]{3,2,1,0:T(8,128)(2,1)} %bitcast.26), calls=%async_computation.1 | async-start | bytes 524288 | tf_op jit(solution)/shard_map/all_to_all | solution.py:74
Sparse Core Ops, SparseCore 0:
  49.6 24.2 reduce-scatter.1
where the time goes:
time: 100 us
  blocking collectives  68.6 us (69%)
  between operations  14.3 us (14%)
  local copies, waits for them, and re-layouts  7.74 us (8%)
  other arithmetic  3.79 us (4%)
  starting transfers between devices  3.44 us (3%)
  matrix products  2.14 us (2%)
    psum x1, blocking collectives, body(): pivot_rows = lax.psum(picked, 'rows').astype(jnp.bfloat16)  37.4 us
    psum x1, blocking collectives, body(): pivot_diag = lax.psum(diag_terms, ('rows', 'cols', 'sub'))  31.2 us
    unnamed x25, local copies, waits for them, and re-layouts  4.02 us
    all_to_all x1, starting transfers between devices, body(): lax.all_to_all(outgoing, 'rows', split_axis=0, concat_axis=0, tiled=True)  3.4 us
  transfers between devices with their start and end apart: 2, of which 0 were waited for; matrix products, arithmetic and copies ran while one was open for 6% of the time, Pallas kernels for 0%

commit v1 on v0

--- a/solution.py
+++ b/solution.py
@@ -52,7 +52,7 @@
     clamped = jnp.clip(band_pivots, 0, band_rows - 1)
     taken = jnp.take(stored_vectors, clamped, axis=1).astype(jnp.float32)
     picked = jnp.where(inside[None, :], taken, jnp.float32(0.0))
-    pivot_rows = lax.psum(picked, "rows").astype(jnp.bfloat16)
+    pivot_rows = jnp.sum(lax.all_gather(picked, "rows"), axis=0).astype(jnp.bfloat16)
     kinds = jnp.arange(shell_norms.shape[0], dtype=jnp.int32)
     factor = jnp.sum(
         jnp.where(shell_tags[..., None] == kinds, shell_norms, jnp.float32(0.0)), axis=-1

time: 100 us -> 133 us (1.33)
  waiting for transfers between devices: 0.02 us -> 64.2 us
  blocking collectives: 68.6 us -> 33.4 us
  other arithmetic: 3.79 us -> 5.92 us
    all_gather x0 -> x1, waiting for transfers between devices: none -> 64.1 us  [body(): lax.all_gather(picked, 'rows')]
    psum x1 -> x0, blocking collectives: 37.4 us -> none  [body(): pivot_rows = lax.psum(picked, 'rows').astype(jnp.bfloat16)]
    psum x1, blocking collectives: 31.2 us -> 33.4 us  [body(): pivot_diag = lax.psum(diag_terms, ('rows', 'cols', 'sub'))]
    reduce_sum x0 -> x1, other arithmetic: none -> 2.13 us  [body(): jnp.sum(lax.all_gather(picked, 'rows'), axis=0).astype(jnp.bfloat16)]
    unnamed x25 -> x26, local copies, waits for them, and re-layouts: 4.02 us -> 4.04 us
  transfers between devices with their start and end apart: 2 -> 3, of which waited for: 0 -> 1; matrix products, arithmetic and copies ran while one was open for 6% -> 5% of each run, Pallas kernels for 0% -> 0%
where the time goes in v1:
time: 133 us; the launch traced here: 132 us
  waiting for transfers between devices  64.2 us (48%)
  blocking collectives  33.4 us (25%)
  between operations  14.3 us (11%)
  local copies, waits for them, and re-layouts  8.91 us (7%)
  other arithmetic  5.92 us (4%)
  starting transfers between devices  3.48 us (3%)
  matrix products  2.14 us (2%)
    all_gather x1, waiting for transfers between devices, body(): lax.all_gather(picked, 'rows')  64.1 us
    psum x1, blocking collectives, body(): pivot_diag = lax.psum(diag_terms, ('rows', 'cols', 'sub'))  33.4 us
    unnamed x26, local copies, waits for them, and re-layouts  4.04 us
    all_to_all x1, starting transfers between devices, body(): lax.all_to_all(outgoing, 'rows', split_axis=0, concat_axis=0, tiled=True)  3.4 us
  transfers between devices with their start and end apart: 3, of which 1 were waited for; matrix products, arithmetic and copies ran while one was open for 5% of the time, Pallas kernels for 0%

profile of v1, /device:TPU:0, one launch (start us, length us, event | category | flops | bytes accessed | tf_op | source)
XLA Modules:
  0.0 132.3 jit_solution(8939198171177577989)
XLA Ops:
  7.2 0.0 all-gather.2.cloned.1.call-start
  7.2 0.0 copy-start.6
  7.2 1.7 %copy.28 = bf16[768,1024]{0,1:T(8,128)(2,1)S(1)} copy(bf16[768,1024]{1,0:T(8,128)(2,1)} %param.9) | data formatting | bytes 3145728 | tf_op args[0]
  9.0 0.0 copy-done.6
  9.0 1.2 gather_fusion
  10.2 0.0 copy-start.7
  10.2 0.0 copy-start.8
  10.2 0.0 copy-start.2
  10.2 0.2 convert_select_fusion
  10.4 0.0 copy-start
  10.4 0.0 copy-start.4
  10.4 1.1 copy.29
  11.6 0.0 all-gather.2.cloned.1.call-update
  11.6 0.0 reduce-scatter.2.cloned.1.call-start
  11.7 0.0 copy-done.7
  11.7 0.0 copy-done.8
  11.7 0.1 select_reduce_fusion.1
  11.8 0.0 copy-done.2
  11.8 0.1 fusion.1
  11.9 0.2 copy.35
  12.1 0.0 copy-done
  12.1 0.6 dynamic_slice.9
  12.7 0.0 copy-done.4
  12.7 0.2 dynamic-slice_reduce_fusion
  12.9 0.7 iota_compare_fusion.6
  13.6 0.2 convert_reduce_fusion.1
  13.8 0.0 copy-start.1
  13.8 64.1 %all-gather.2.cloned.1.call-done = f32[4,768,256]{2,1,0:T(8,128)} async-done(((f32[1,768,256]{2,1,0:T(8,128)}), f32[4,768,256]{2,1,0:T(8,128)}) %all-gather.2.cloned.1.call-update) | async-done | bytes 3145744 | tf_op jit(solution)/shard_map/all_gather | solution.py:55
  77.9 2.1 %reduce_sum.54 = bf16[768,256]{1,0:T(8,128)(2,1)S(1)} reduce(f32[4,768,256]{2,1,0:T(8,128)} %all-gather.2.cloned.1.call-done, f32[]{:T(128)} %constant.124.clone.1), dimensions={0}, to_apply=%region_0.1 | reduce | flops 589824 | bytes 3538948 | tf_op jit(solution)/shard_map/reduce_sum | solution.py:55
  80.1 0.2 copy.34
  80.2 0.0 copy-done.1
  80.2 1.6 %convolution_bitcast_fusion = f32[1024,256]{0,1:T(8,128)} fusion(bf16[768,1024]{1,0:T(8,128)(2,1)S(1)} %copy-done.1, bf16[768,256]{0,1:T(8,128)(2,1)S(1)} %copy.34), kind=kOutput, calls=%fused_computation.5 | convolution fusion | flops 402653184 | bytes 3014656 | tf_op jit(solution)/shard_map/dot_general | solution.py:102
  81.8 0.0 copy-start.5
  81.8 0.0 copy-start.3
  81.8 0.0 reduce-scatter.2.cloned.1.call-update
  81.8 0.3 convolution_convert_fusion
  82.1 0.7 copy.39
  82.9 3.4 %all-to-all-start = ((bf16[4,1,128,256]{3,2,1,0:T(8,128)(2,1)}), bf16[4,1,128,256]{3,2,1,0:T(8,128)(2,1)S(1)}, u32[]{:S(2)}, u32[]{:S(2)}) async-start(bf16[4,1,128,256]{3,2,1,0:T(8,128)(2,1)} %bitcast.30), calls=%async_computation.1 | async-start | bytes 524288 | tf_op jit(solution)/shard_map/all_to_all | solution.py:74
  86.3 0.1 copy.31
  86.4 0.6 gather_fusion.2
  87.0 0.6 gather_fusion.1
  87.6 0.1 compare_and_fusion
  87.7 0.2 convert_reduce_fusion
  87.9 0.0 copy-done.5
  88.0 0.1 select_reduce_fusion
  88.1 33.4 %psum.7 = f32[256]{0:T(256)S(1)} all-reduce(f32[256]{0:T(256)S(1)} %select_reduce_fusion), channel_id=1, replica_groups=mesh['groups'=2,'rows'=4,'cols'=2,'sub'=2] {'rows','cols','sub'}, use_global_device_ids=true, to_apply=%region_3.4 | all-reduce | flops 256 | bytes 2048 | tf_op jit(solution)/shard_map/psum | solution.py:49
  121.4 0.0 copy-done.3
  121.4 0.1 copy.27
  121.6 0.1 add_select_fusion.2
  121.6 0.2 fusion.4
  121.8 0.0 all-to-all-done
  121.8 0.2 copy.37
  122.0 0.3 convolution_convert_fusion.1
  122.3 0.7 reshape.383
  123.0 0.0 reduce-scatter.2.cloned.1.call-done
  123.0 1.1 multiply_reduce_fusion
  124.1 0.8 copy.33
  124.9 0.6 sub.35
  (11 shorter events, 0.1 us)
Async XLA Ops:
  7.2 70.8 %all-gather.2.cloned.1.call-start = ((), (), s32[]{:S(2)}) async-start(), calls=%async_computation.2 | async-start | bytes 3932160 | tf_op jit(solution)/shard_map/all_gather | solution.py:55
  7.2 1.7 %copy-start.6 = (s32[256]{0:T(256)S(1)}, s32[256]{0:T(256)}, u32[]{:S(2)}) copy-start(s32[256]{0:T(256)} %param.11) | copy-start | bytes 3076
  10.2 1.5 %copy-start.7 = (s32[4,128]{1,0:T(4,128)S(1)}, s32[4,128]{1,0:T(4,128)}, u32[]{:S(2)}) copy-start(s32[4,128]{1,0:T(4,128)} %param.14) | copy-start | bytes 6148
  10.2 1.5 %copy-start.8 = (f32[4]{0:T(128)S(1)}, f32[4]{0:T(128)}, u32[]{:S(2)}) copy-start(f32[4]{0:T(128)} %param.17) | copy-start | bytes 52
  10.2 1.6 %copy-start.2 = (bf16[4,128,256]{2,1,0:T(8,128)(2,1)S(1)}, bf16[4,128,256]{2,1,0:T(8,128)(2,1)}, u32[]{:S(2)}) copy-start(bf16[4,128,256]{2,1,0:T(8,128)(2,1)} %param.13) | copy-start | bytes 786436
  10.4 1.7 %copy-start = (s32[16]{0:T(128)S(1)}, s32[16]{0:T(128)}, u32[]{:S(2)}) copy-start(s32[16]{0:T(128)} %param.16) | copy-start | bytes 196
  10.4 2.3 %copy-start.4 = (s32[16,4]{0,1:T(4,128)S(1)}, s32[16,4]{0,1:T(4,128)}, u32[]{:S(2)}) copy-start(s32[16,4]{0,1:T(4,128)} %param.15) | copy-start | bytes 772
  11.6 111.4 %reduce-scatter.2.cloned.1.call-start = ((), (), s32[]{:S(2)}) async-start(), calls=%async_computation.3 | async-start | bytes 1310720 | tf_op jit(solution)/shard_map/reduce_scatter | solution.py:101
  13.8 66.4 %copy-start.1 = (bf16[768,1024]{1,0:T(8,128)(2,1)S(1)}, bf16[768,1024]{1,0:T(8,128)(2,1)}, u32[]{:S(2)}) copy-start(bf16[768,1024]{1,0:T(8,128)(2,1)} %param.9) | copy-start | bytes 4718596
  81.8 6.1 %copy-start.5 = (f32[256]{0:T(256)S(1)}, f32[256]{0:T(256)}, u32[]{:S(2)}) copy-start(f32[256]{0:T(256)} %param.12) | copy-start | bytes 3076
  81.8 39.6 %copy-start.3 = (bf16[256,256]{1,0:T(8,128)(2,1)S(1)}, bf16[256,256]{1,0:T(8,128)(2,1)}, u32[]{:S(2)}) copy-start(bf16[256,256]{1,0:T(8,128)(2,1)} %param.10) | copy-start | bytes 393220
  82.9 38.9 %all-to-all-start = ((bf16[4,1,128,256]{3,2,1,0:T(8,128)(2,1)}), bf16[4,1,128,256]{3,2,1,0:T(8,128)(2,1)S(1)}, u32[]{:S(2)}, u32[]{:S(2)}) async-start(bf16[4,1,128,256]{3,2,1,0:T(8,128)(2,1)} %bitcast.30), calls=%async_computation.1 | async-start | bytes 524288 | tf_op jit(solution)/shard_map/all_to_all | solution.py:74
Sparse Core Ops, SparseCore 0:
  11.7 66.1 all-gather.1
  82.0 23.5 reduce-scatter.1
